TPU v7x, 32 devices: a 4x4x1 block of a 4x4x8 slice. The times are simulated.
32 devices in a mesh: layer: 1 (over z), tensor: 32 (over y, x, core).
Axes of the slice: x: 4, y: 4, z: 1, core: 2. Of those that a mesh axis runs over, the one named last changes fastest.
The devices are a block of a 4x4x8 slice.
Arguments:
- gradient: bfloat16 [4096, 8192], P('layer', 'tensor')
- left_stat: float32 [4096, 4096], P(('layer', 'tensor'))
- right_stat: float32 [8192, 8192], P(('layer', 'tensor'))
- left_root: bfloat16 [4096, 4096], P(('layer', 'tensor'))
- right_root: bfloat16 [8192, 8192], P(('layer', 'tensor'))
Outputs:
- output 1: float32 [4096, 4096], P(('layer', 'tensor'))
- output 2: float32 [8192, 8192], P(('layer', 'tensor'))
- output 3: float32 [4096, 8192], P('layer', 'tensor')
All inputs are finite; a program needn't handle non-finite values.
Results may differ from a plain program's by a relative error of at most 0.001.
Values are sent between devices in bfloat16 or wider.
A program may use at most 768 MiB of HBM per device.

v0:
```python
import functools
import math

import jax
import jax.numpy as jnp
from jax import lax
from jax.experimental import pallas as pl
from jax.experimental.pallas import tpu as pltpu
from jax.sharding import PartitionSpec as P

EMA_DECAY = 0.9
CORES = 2
MESH = pl.DeviceIdType.MESH

ORDER = [(int(a), int(b)) for a, b in zip("0310020311322312", "0003102313131222")]
def parcels(code):
    digits = [int(d) for d in code]
    return [((a, b), h) for a, b, h in zip(digits[0::3], digits[1::3], digits[2::3])]


UP = parcels("030031330131020331130230231320120220")
UP_ON = {0: parcels("030"), 2: parcels("330"), 6: parcels("130"), 7: parcels("230")}
DOWN = parcels("011010111310021110311211210321121221")
DOWN_ON = {0: parcels("011"), 6: parcels("311111"), 7: parcels("211")}
ROUNDS = len(UP)
FIRST_UP = parcels("300301200")
FIRST_DOWN = parcels("101100201")
GRAD_ROUND_STEP = [2, 2, 8, 10, 12, 14, 17, 20, 22, 26, 28, 30]
LAST_FORWARD = 7
SIDE_UP, SIDE_DOWN = 9, 10
ASIDE = 36
ROOT_START_STEP = 28
ROOT_ACROSS_STEP = 30
RELAY_STEP = 32
LATE = (2, 12, 14, 22, 26, 28, 30)


def round_of(name, offset, half):
    a, b = offset
    table, da, db = {"f+": (FIRST_UP, 3, 0), "f-": (FIRST_DOWN, 1, 0), "s+": (UP, 0, 3), "s-": (DOWN, 0, 1)}[name]
    return table.index((((a + da) % 4, (b + db) % 4), half))


def packed(values):
    return [sum(v << (2 * i) for i, v in enumerate(values[j:j + 8])) for j in (0, 8)]


FIRST_CODE = packed([o[0] for o in ORDER])
SECOND_CODE = packed([o[1] for o in ORDER])


def lookup(code, e):
    word = code[0] + (e // 8) * (code[1] - code[0])
    return lax.shift_right_logical(word, 2 * (e % 8)) & 3


ROOT_ORDER = [(0, 0), (3, 0), (1, 0), (0, 1), (2, 0), (3, 1), (1, 1), (2, 1)]
ROOT_Y = sum(o[0] << (2 * i) for i, o in enumerate(ROOT_ORDER))
FAR_TURN, LAST_TURN, TWIN_LAST, TWIN_TURN = 5, 7, 9, 10
ROOT_X = sum(o[1] << (2 * i) for i, o in enumerate(ROOT_ORDER))


def kernel(n, side, g_ref, l_ref, r_ref, lr_ref, rr_ref, lo_ref, ro_ref, do_ref, gfull,
           rr, gt, acc, gbuf, rhs, xx, lroot, relay, lent,
           g_recv, g_send, load_sem, init_sem, l_recv, relay_recv, x_recv, d_recv, l_send, x_send, d_send, x_gone):
    _, half_rows, cols = g_ref.shape
    rows = 2 * half_rows
    lrows = l_ref.shape[0]
    tile = min(1024, half_rows)
    aside_rows = half_rows * ASIDE // 128

    me = lax.axis_index("tensor")
    c = me % CORES
    chip = me // CORES
    x, y = chip % side, chip // side
    f = x + c * (y - x)
    s = y + c * (x - y)
    fstep = CORES + c * CORES * (side - 1)
    sstep = CORES * side - c * CORES * (side - 1)
    twin = me + 1 - 2 * c

    def index(df, ds):
        return ((f + df) % side) * fstep + ((s + ds) % side) * sstep + c

    def twin_index(df, ds):
        return ((s + df) % side) * sstep + ((f + ds) % side) * fstep + 1 - c

    peers = {"f+": index(1, 0), "f-": index(3, 0), "s+": index(0, 1), "s-": index(0, 3), "twin": twin}

    class Gather:
        def __init__(self, own, full, recv, send):
            self.own, self.full, self.recv, self.send_sem = own, full, recv, send
            self.sent = 0

        def copy(self, name, offset, half, part=None, turn=None):
            b = index(*offset)
            src = self.own.at[half] if offset == (0, 0) else self.full.at[2 * b + half]
            dst = self.full.at[2 * b + half]
            if part is not None:
                src, dst = src.at[pl.ds(*part)], dst.at[pl.ds(*part)]
            if turn is None:
                turn = ROUNDS + b // CORES if name == "twin" else round_of(name, offset, half)
            return pltpu.make_async_remote_copy(
                src_ref=src, dst_ref=dst, send_sem=self.send_sem.at[0], recv_sem=self.recv.at[turn],
                device_id={"tensor": peers[name]}, device_id_type=MESH)

        def send(self, name, offset, half):
            self.sent += 1
            self.copy(name, offset, half).start()

        def wait(self, turn, count):
            taken = self.full.at[pl.ds(0, count)]
            pltpu.make_async_copy(taken, taken, self.recv.at[turn]).wait()

        def start(self):
            for half in (0, 1):
                for name in ("f+", "s+"):
                    self.send(name, (0, 0), half)
                for name in ("f-", "s-"):
                    self.send(name, (0, 0), 1 - half)
            for half in (0, 1):
                self.send("twin", (0, 0), half)

        def round(self, r):
            first = r < len(FIRST_UP)
            self.wait(r, 4 if first else 2)
            if first:
                above, below = FIRST_UP[r], FIRST_DOWN[r]
                if r == 0:
                    self.send("f+", *above)
                    self.send("f-", *below)
                self.send("s+", *above)
                self.send("s-", *below)
                self.send("s+", *below)
                self.send("s-", *above)
                self.send("twin", *above)
                self.send("twin", *below)
            for name, table in (("s+", UP_ON), ("s-", DOWN_ON)):
                for parcel in table.get(r, ()):
                    if r == LAST_FORWARD:
                        self.forward_last(name, *parcel)
                    else:
                        self.send(name, *parcel)
            if r == SIDE_UP:
                self.aside("f+", *UP[r])
            if r == SIDE_DOWN:
                self.aside("f-", *DOWN[r])
            self.send("twin", *UP[r])
            self.send("twin", *DOWN[r])

        def forward_last(self, name, offset, half):
            self.sent += 1
            pl.when(c == 0)(lambda: self.copy(name, offset, half, part=(0, half_rows - aside_rows)).start())
            pl.when(c == 1)(lambda: self.copy(name, offset, half).start())

        def aside(self, name, offset, half):
            part = (half_rows - aside_rows, aside_rows)
            pl.when(c == 0)(lambda: self.copy(name, offset, half, part=part, turn=ROUNDS - 1).start())

        def drain(self):
            whole = self.full.at[pl.ds(0, self.sent)]
            pltpu.make_async_copy(whole, whole, self.send_sem.at[0]).wait()

    grad = Gather(g_ref, gfull, g_recv, g_send)

    def block_of(k):
        e, other = k // 2, k % 2
        df, ds = lookup(FIRST_CODE, e), lookup(SECOND_CODE, e)
        mine = index(df, ds)
        return mine + other * (twin_index(df, ds) - mine)

    def load(gather, buf, k, sem):
        b = block_of(k)
        return pltpu.make_async_copy(gather.full.at[pl.ds(2 * b, 2)], buf.at[k % 2], sem.at[k % 2])

    def one_of(k, values):
        found = k == values[0]
        for v in values[1:]:
            found = found | (k == v)
        return found

    def steps(gather, buf, sem, round_step, early, between, after, work):
        def at_steps(k, actions):
            for at, action in actions:
                pl.when(k == at)(action)

        def step(k, carry):
            at_steps(k, early)

            @pl.when((k % 2 == 1) & (k < n))
            def _():
                gather.wait(ROUNDS + block_of(k) // CORES, 2)

            @pl.when(jnp.logical_not(one_of(k, LATE)) & (k < n))
            def _():
                load(gather, buf, k, sem).start()
            load(gather, buf, k - 1, sem).wait()
            work((k - 1) % 2, block_of(k - 1))
            at_steps(k, between)
            for r in range(ROUNDS):
                @pl.when(k == round_step[r])
                def _():
                    gather.round(r)
            at_steps(k, after)

            @pl.when(one_of(k, LATE))
            def _():
                load(gather, buf, k, sem).start()
            return carry
        lax.fori_loop(1, n + 1, step, 0)

    barrier = pltpu.get_barrier_semaphore()
    for peer in peers.values():
        pl.semaphore_signal(barrier, inc=1, device_id={"tensor": peer}, device_id_type=MESH)

    first = [
        pltpu.make_async_copy(rr_ref, rr, init_sem.at[0]),
        pltpu.make_async_copy(r_ref, ro_ref, init_sem.at[1]),
        pltpu.make_async_copy(l_ref, lo_ref, init_sem.at[2]),
        pltpu.make_async_copy(lr_ref, lroot.at[pl.ds(2 * ((y * (side // 2) + x // 2) * CORES + c), 2)], init_sem.at[3]),
    ]
    own_load = pltpu.make_async_copy(g_ref, gbuf.at[0], load_sem.at[0])
    own_load.start()

    pl.semaphore_wait(barrier, len(peers))
    grad.start()
    for copy in first:
        copy.start()

    acc[...] = jnp.zeros_like(acc)
    own_load.wait()
    for h in (0, 1):
        gt[:, h * half_rows:(h + 1) * half_rows] = gbuf[0, h].T
    for copy in first:
        copy.wait()
    own_load.start()

    per_half = half_rows // tile

    def grad_work(slot, b):
        at = pl.multiple_of(b * cols, cols)
        rhs[:cols] = rr[:, pl.ds(at, cols)]
        rhs[cols:] = gbuf[slot, me // (n // 2), pl.ds(pl.multiple_of((me % (n // 2)) * lrows, lrows), lrows), :]

        def rows_step(t, carry):
            left = gbuf[slot, t // per_half, pl.ds(pl.multiple_of((t % per_half) * tile, tile), tile), :]
            out = pl.ds(pl.multiple_of(t * tile, tile), tile)
            acc[out, :] += lax.dot_general(left, rhs[...], (((1,), (1,)), ((), ())), preferred_element_type=jnp.float32)
            return carry
        lax.fori_loop(0, 2 * per_half, rows_step, 0)
        prod = jnp.dot(gt[:, :half_rows], gbuf[slot, 0], preferred_element_type=jnp.float32)
        prod += jnp.dot(gt[:, half_rows:], gbuf[slot, 1], preferred_element_type=jnp.float32)
        ro_ref[:, pl.ds(at, cols)] = EMA_DECAY * ro_ref[:, pl.ds(at, cols)] + (1.0 - EMA_DECAY) * prod


    dx = 1 - 2 * c
    helper = (y * side + (x + dx + side) % side) * CORES + c
    client = (y * side + (x - dx + side) % side) * CORES + c
    up = (((y + 1) % side) * side + x) * CORES + c
    down = (((y + side - 1) % side) * side + x) * CORES + c
    half_count, root_half, _ = lroot.shape
    pieces = ((0, root_half - root_half // 4), (root_half - root_half // 4, root_half // 4))

    def root_block(dy, q, p=0):
        oy, ox = (y + dy) % side, (x + 2 * q) % side
        core = c + p * (1 - 2 * c)
        return (oy * (side // 2) + ox // 2) * CORES + core, (oy * side + ox) * CORES + core

    def root_copy(peer, place, half, src=None, dst=None, recv=None, part=None, across=0):
        here = lroot.at[2 * place + half]
        if part is not None:
            here = here.at[pl.ds(*pieces[part])]
        if peer is twin and recv is None:
            recv = l_recv.at[TWIN_TURN + place // CORES]
        return pltpu.make_async_remote_copy(
            src_ref=here if src is None else src, dst_ref=here if dst is None else dst, send_sem=l_send.at[across],
            recv_sem=l_recv.at[recv] if isinstance(recv, int) else recv, device_id={"tensor": peer}, device_id_type=MESH)

    sent = [0, 0]

    def root_send(peer, place, half, part=None, across=0, **kw):
        sent[across] += root_half if part is None else pieces[part][1]
        root_copy(peer, place, half, part=part, across=across, **kw).start()

    def uncounted(action):
        before = list(sent)
        action()
        sent[:] = before

    def pair_wait(pair, sem):
        pltpu.make_async_copy(pair, pair, sem).wait()

    own_place, _ = root_block(0, 0)
    far_place, _ = root_block(0, 1)
    passing = (y * (side // 2) + ((x - dx + side) % side) // 2) * CORES + c

    def root_start_across():
        for half in (0, 1):
            root_send(helper, own_place, half, across=1, src=lr_ref.at[half], dst=relay.at[half], recv=relay_recv.at[half])

    def root_start():
        for half in (0, 1):
            root_send(up, own_place, half, src=lr_ref.at[half], recv=half)
            root_send(down, own_place, 1 - half, src=lr_ref.at[1 - half], recv=half)
        for half in (0, 1):
            root_send(twin, own_place, half, src=lr_ref.at[half])

    def root_relay(half):
        root_copy(helper, own_place, half, src=lr_ref.at[half], dst=relay.at[half], recv=relay_recv.at[half]).wait_recv()
        root_send(helper, passing, half, across=1, src=relay.at[half], recv=FAR_TURN + half)
        root_send(twin, passing, half, across=1, src=relay.at[half], dst=relay.at[2 + half], recv=relay_recv.at[2])

    def passed_rows(p):
        if p:
            pair_wait(relay.at[pl.ds(2, 2)], relay_recv.at[2])
        source = (y * side + (x - (1 - 2 * p) * dx + side) % side) * CORES + c + p * (1 - 2 * c)
        left = relay[2 * p:2 * p + 2].reshape(lrows, rows)
        do_ref[rows_of(source), :] = jnp.dot(left, xx[0], preferred_element_type=jnp.float32)

    def root_far():
        for half in (0, 1):
            pltpu.make_async_copy(lroot.at[0], lroot.at[0], l_recv.at[FAR_TURN + half]).wait()
            root_send(up, far_place, half, recv=3 + half)
            root_send(twin, far_place, half)
        for half in (1, 0):
            root_send(down, far_place, half, recv=4 - half)

    def root_round(r):
        q, stage = r // 3, r % 3
        pair_wait(lroot.at[pl.ds(0, 2)], l_recv.at[r])
        if stage == 2:
            below = above = root_block(2, q)[0]
        else:
            below, above = root_block(side - 1, q)[0], root_block(1, q)[0]
        if stage == 0:
            for peer, place, half in ((up, below, 0), (down, above, 1)):
                if q == 0:
                    root_send(peer, place, half, recv=2)
                else:
                    for part in (0, 1):
                        root_send(peer, place, half, part=part, recv=LAST_TURN + part)
        root_send(twin, below, stage % 2)
        root_send(twin, above, 1 - stage % 2)

    last_place, last_device = root_block(2, 1)
    twin_place, twin_device = root_block(2, 1, 1)

    def root_last(part):
        pair_wait(lroot.at[pl.ds(0, 2), pl.ds(*pieces[part])], l_recv.at[LAST_TURN + part])
        for half in (0, 1):
            root_send(twin, last_place, half, part=part, recv=TWIN_LAST if part else None)

    def root_last_twin(part):
        pair = lroot.at[pl.ds(2 * twin_place, 2), pl.ds(*pieces[part])]
        pair_wait(pair, l_recv.at[TWIN_LAST if part else TWIN_TURN + twin_place // CORES])

    steps(grad, gbuf, load_sem, GRAD_ROUND_STEP, [(RELAY_STEP, lambda: root_relay(0))],
          [(ROOT_ACROSS_STEP, root_start_across), (ROOT_ACROSS_STEP, lambda: pl.when(c == 1)(lambda: uncounted(root_start)))],
          [(ROOT_START_STEP, lambda: pl.when(c == 0)(root_start))], grad_work)

    side_cols = cols // 2

    def x_copy(h):
        at = pl.ds(h * side_cols, side_cols)
        return pltpu.make_async_remote_copy(
            src_ref=xx.at[0, :, at], dst_ref=xx.at[1, :, at], send_sem=x_send.at[h], recv_sem=x_recv.at[h],
            device_id={"tensor": helper}, device_id_type=MESH)

    xx[0] = acc[:, :cols].astype(jnp.bfloat16)
    root_relay(1)
    x_copy(0).start()
    x_copy(1).start()
    root_round(0)

    def left_step(t, carry):
        at = pl.ds(pl.multiple_of(t * lrows, lrows), lrows)
        lo_ref[:, at] = EMA_DECAY * lo_ref[:, at] + (1.0 - EMA_DECAY) * acc[at, cols:].T
        return carry
    lax.fori_loop(0, rows // lrows, left_step, 0)

    def at_step(i):
        e, p = i // 2, i % 2
        dy = lax.shift_right_logical(ROOT_Y, 2 * e) & 3
        q = lax.shift_right_logical(ROOT_X, 2 * e) & 3
        return root_block(dy, q, p)

    def twin_wait(i, place):
        @pl.when(i % 2 == 1)
        def _():
            pair_wait(lroot.at[pl.ds(2 * place, 2)], l_recv.at[TWIN_TURN + place // CORES])

    def product(place, which):
        left = lroot[pl.ds(2 * place, 2)].reshape(lrows, rows)
        return jnp.dot(left, xx[which], preferred_element_type=jnp.float32)

    def rows_of(device):
        return pl.ds(pl.multiple_of(device * lrows, lrows), lrows)

    def own_rows(i):
        place, device = at_step(i)
        do_ref[rows_of(device), :] = product(place, 0)

    def lent_copy(i, device):
        return pltpu.make_async_remote_copy(
            src_ref=lent.at[i], dst_ref=do_ref.at[rows_of(device)], send_sem=d_send.at[0], recv_sem=d_recv.at[0],
            device_id={"tensor": client}, device_id_type=MESH)

    def lent_rows(i):
        place, device = at_step(i)
        lent[i] = product(place, 1)
        lent_copy(i, device).start()

    def lent_side(i, h):
        place, _ = at_step(i)
        at = pl.ds(h * side_cols, side_cols)
        left = lroot[pl.ds(2 * place, 2)].reshape(lrows, rows)
        lent[i, :, at] = jnp.dot(left, xx[1, :, at], preferred_element_type=jnp.float32)

    def lent_side_copy(i, h):
        _, device = at_step(i)
        at = pl.ds(h * side_cols, side_cols)
        return pltpu.make_async_remote_copy(
            src_ref=lent.at[i, :, at], dst_ref=do_ref.at[rows_of(device), at], send_sem=d_send.at[0], recv_sem=d_recv.at[0],
            device_id={"tensor": client}, device_id_type=MESH)

    def loop(lo, hi, body):
        def step(i, carry):
            body(i)
            return carry
        lax.fori_loop(lo, hi, step, 0)

    def first_own(i):
        @pl.when(i == 2)
        def _():
            root_far()
            root_round(1)

        @pl.when(i == 8)
        def _():
            root_round(2)
        twin_wait(i, at_step(i)[0])
        own_rows(i)

    loop(0, 10, first_own)
    passed_rows(0)
    passed_rows(1)
    x_copy(0).wait_recv()
    def lent_step(j):
        return j + (j + 7) // 8 + j // 5

    loop(0, 8, lambda j: lent_side(lent_step(j), 0))
    x_copy(0).wait_send()
    x_copy(1).wait_send()
    pl.semaphore_signal(x_gone, inc=1, device_id={"tensor": twin}, device_id_type=MESH)
    pl.semaphore_wait(x_gone, 1)
    loop(0, 8, lambda j: lent_side_copy(lent_step(j), 0).start())
    root_round(3)
    x_copy(1).wait_recv()

    def second_side(j):
        i = lent_step(j)
        lent_side(i, 1)
        lent_side_copy(i, 1).start()
    loop(0, 8, second_side)
    root_round(4)

    def both(i):
        twin_wait(i, at_step(i)[0])
        lent_rows(i)
        own_rows(i)
    loop(10, 14, both)

    def lent_piece(i, place, device, part):
        first, count = pieces[part]
        left = jnp.concatenate([lroot[2 * place, pl.ds(first, count), :], lroot[2 * place + 1, pl.ds(first, count), :]], axis=0)
        prod = jnp.dot(left, xx[1], preferred_element_type=jnp.float32)
        for half in (0, 1):
            at = half * root_half + first
            lent[i, pl.ds(at, count), :] = prod[half * count:(half + 1) * count]
            pltpu.make_async_remote_copy(
                src_ref=lent.at[i, pl.ds(at, count)], dst_ref=do_ref.at[pl.ds(pl.multiple_of(device * lrows, lrows) + at, count)],
                send_sem=d_send.at[0], recv_sem=d_recv.at[0], device_id={"tensor": client}, device_id_type=MESH).start()

    def own_piece(part):
        root_last(part)
        lent_piece(14, last_place, last_device, part)

    def twin_piece(part):
        root_last_twin(part)
        lent_piece(15, twin_place, twin_device, part)

    @pl.when(c == 0)
    def _():
        own_piece(0)
        own_piece(1)
        twin_piece(0)
        twin_piece(1)

    @pl.when(c == 1)
    def _():
        uncounted(lambda: own_piece(0))
        twin_piece(0)
        twin_piece(1)
        uncounted(lambda: own_piece(1))

    loop(14, 16, own_rows)

    grad.drain()
    for across, count in enumerate(sent):
        whole = lroot.at[pl.ds(0, count // root_half)]
        pltpu.make_async_copy(whole, whole, l_send.at[across]).wait()
    given = lent.at[pl.ds(0, half_count // 2 - 2)]
    pltpu.make_async_copy(given, given, d_send.at[0]).wait()
    pltpu.make_async_copy(given, given, d_recv.at[0]).wait()


def store_kernel(*refs):
    count = (len(refs) - 1) // 2
    sems = refs[-1]
    pieces = 8
    for i in range(count):
        src, dst = refs[i], refs[count + i]
        step = src.shape[0] // pieces
        for j in range(pieces):
            part = pl.ds(j * step, step)
            pltpu.make_async_copy(src.at[part], dst.at[part], sems.at[i]).start()
    for i in range(count):
        pltpu.make_async_copy(refs[i], refs[count + i], sems.at[i]).wait()


def solution(mesh):
    row_spec = P(("layer", "tensor"), None)
    col_spec = P("layer", "tensor")
    n = mesh.shape["tensor"]
    side = math.isqrt(n // CORES)

    def local_step(g, l, r, lr, rr):
        rows, cols = g.shape
        lrows = l.shape[0]
        kept = n // 2
        hbm = pl.BlockSpec(memory_space=pltpu.HBM)
        vmem = pl.BlockSpec(memory_space=pltpu.VMEM)
        operands = [g.reshape(2, rows // 2, cols), l, r, lr.reshape(2, lrows // 2, rows), rr]
        left_new, right_new, direction, _ = pl.pallas_call(
            functools.partial(kernel, n, side),
            name="shampoo",
            out_shape=[
                pltpu.VMEM(l.shape, jnp.float32),
                pltpu.VMEM(r.shape, jnp.float32),
                pltpu.VMEM(g.shape, jnp.float32),
                pltpu.HBM((2 * n, rows // 2, cols), jnp.bfloat16),
            ],
            in_specs=[hbm] * 5,
            out_specs=[vmem, vmem, vmem, hbm],
            scratch_shapes=[
                pltpu.VMEM(rr.shape, jnp.bfloat16),
                pltpu.VMEM((cols, rows), jnp.bfloat16),
                pltpu.VMEM((rows, cols + lrows), jnp.float32),
                pltpu.VMEM((2, 2, rows // 2, cols), jnp.bfloat16),
                pltpu.VMEM((cols + lrows, cols), jnp.bfloat16),
                pltpu.VMEM((2, rows, cols), jnp.bfloat16),
                pltpu.VMEM((2 * kept, lrows // 2, rows), jnp.bfloat16),
                pltpu.VMEM((4, lrows // 2, rows), jnp.bfloat16),
                pltpu.VMEM((kept, lrows, cols), jnp.float32),
                pltpu.SemaphoreType.DMA((ROUNDS + n // 2,)),
                pltpu.SemaphoreType.DMA((1,)),
                pltpu.SemaphoreType.DMA((2,)),
                pltpu.SemaphoreType.DMA((4,)),
                pltpu.SemaphoreType.DMA((TWIN_TURN + kept // 2,)),
                pltpu.SemaphoreType.DMA((3,)),
                pltpu.SemaphoreType.DMA((2,)),
                pltpu.SemaphoreType.DMA((1,)),
                pltpu.SemaphoreType.DMA((2,)),
                pltpu.SemaphoreType.DMA((2,)),
                pltpu.SemaphoreType.DMA((1,)),
                pltpu.SemaphoreType.REGULAR,
            ],
            compiler_params=pltpu.CompilerParams(collective_id=0, has_side_effects=True, vmem_limit_bytes=48 * 2**20),
            cost_estimate=pl.CostEstimate(flops=2 * rows * cols * (2 * n * cols + 2 * rows), bytes_accessed=2 * n * rows * cols * 3, transcendentals=0),
        )(*[pltpu.with_memory_space_constraint(v, pltpu.HBM) for v in operands])
        results = [left_new, right_new, direction]
        return pl.pallas_call(
            store_kernel,
            name="store",
            out_shape=[jax.ShapeDtypeStruct(v.shape, v.dtype) for v in results],
            in_specs=[vmem] * 3,
            out_specs=[hbm] * 3,
            scratch_shapes=[pltpu.SemaphoreType.DMA((3,))],
            compiler_params=pltpu.CompilerParams(vmem_limit_bytes=1 * 2**20),
        )(*results)

    return jax.shard_map(local_step, mesh=mesh, in_specs=(col_spec, row_spec, row_spec, row_spec, row_spec), out_specs=(row_spec, row_spec, col_spec), check_vma=False)
```

profile of v0, /device:TPU:97, one launch (start us, length us, event | category | flops | bytes accessed | tf_op | source)
XLA Modules:
  0.0 252.8 jit_solution(15507758334461389638)
XLA Ops:
  0.6 247.0 %shampoo.1 = (f32[128,4096]{1,0:T(8,128)S(1)}, f32[256,8192]{1,0:T(8,128)S(1)}, f32[4096,256]{1,0:T(8,128)S(1)}, bf16[64,2048,256]{2,1,0:T(8,128)(2,1)}) custom-call(bf16[2,2048,256]{2,1,0:T(8,128)(2,1)} %bitcast.2, f32[128,4096]{1,0:T(8,128)} %l_ref.1, f32[256,8192]{1,0:T(8,128)} %r_ref.1, bf16[2,64,4096]{2,1,0:T(8,128)(2,1)} %bitcast.3, ...), custom_call_target="tpu_custom_call" | custom-call | flops 51539607552 | bytes 201326592 | tf_op jit(solution)/shard_map/shampoo/pallas_call | solution.py:544
  247.6 5.2 %store.1 = (f32[128,4096]{1,0:T(8,128)}, f32[256,8192]{1,0:T(8,128)}, f32[4096,256]{1,0:T(8,128)}) custom-call(f32[128,4096]{1,0:T(8,128)S(1)} %get-tuple-element.6.refs_0_, f32[256,8192]{1,0:T(8,128)S(1)} %get-tuple-element.7.refs_1_, f32[4096,256]{1,0:T(8,128)S(1)} %get-tuple-element.8.refs_2_), custom_call_target="tpu_custom_call" | custom-call | tf_op jit(solution)/shard_map/store/pallas_call | solution.py:582
where the time goes:
time: 253 us
  Pallas kernels  252 us (100%)
    pallas_call x1, Pallas kernels, local_step(): pl.pallas_call(functools.partial(kernel, n, side), name='shampoo', out_sh...  247 us
    pallas_call x1, Pallas kernels, local_step(): pl.pallas_call(store_kernel, name='store', out_shape=[jax.ShapeDtypeStruc...  5.19 us

commit v1 on v0

--- a/solution.py
+++ b/solution.py
@@ -56,13 +56,13 @@
 
 ROOT_ORDER = [(0, 0), (3, 0), (1, 0), (0, 1), (2, 0), (3, 1), (1, 1), (2, 1)]
 ROOT_Y = sum(o[0] << (2 * i) for i, o in enumerate(ROOT_ORDER))
-FAR_TURN, LAST_TURN, TWIN_LAST, TWIN_TURN = 5, 7, 9, 10
+FAR_TURN, LAST_TURN, ROOT_TURNS = 5, 7, 9
 ROOT_X = sum(o[1] << (2 * i) for i, o in enumerate(ROOT_ORDER))
 
 
 def kernel(n, side, g_ref, l_ref, r_ref, lr_ref, rr_ref, lo_ref, ro_ref, do_ref, gfull,
            rr, gt, acc, gbuf, rhs, xx, lroot, relay, lent,
-           g_recv, g_send, load_sem, init_sem, l_recv, relay_recv, x_recv, d_recv, l_send, x_send, d_send, x_gone):
+           g_recv, g_send, load_sem, l_recv, relay_recv, x_recv, d_recv, l_send, x_send, d_send, x_gone):
     _, half_rows, cols = g_ref.shape
     rows = 2 * half_rows
     lrows = l_ref.shape[0]
@@ -99,7 +99,7 @@
             if part is not None:
                 src, dst = src.at[pl.ds(*part)], dst.at[pl.ds(*part)]
             if turn is None:
-                turn = ROUNDS + b // CORES if name == "twin" else round_of(name, offset, half)
+                turn = ROUNDS + ORDER.index(offset) if name == "twin" else round_of(name, offset, half)
             return pltpu.make_async_remote_copy(
                 src_ref=src, dst_ref=dst, send_sem=self.send_sem.at[0], recv_sem=self.recv.at[turn],
                 device_id={"tensor": peers[name]}, device_id_type=MESH)
@@ -189,7 +189,7 @@
 
             @pl.when((k % 2 == 1) & (k < n))
             def _():
-                gather.wait(ROUNDS + block_of(k) // CORES, 2)
+                gather.wait(ROUNDS + k // 2, 2)
 
             @pl.when(jnp.logical_not(one_of(k, LATE)) & (k < n))
             def _():
@@ -214,10 +214,10 @@
         pl.semaphore_signal(barrier, inc=1, device_id={"tensor": peer}, device_id_type=MESH)
 
     first = [
-        pltpu.make_async_copy(rr_ref, rr, init_sem.at[0]),
-        pltpu.make_async_copy(r_ref, ro_ref, init_sem.at[1]),
-        pltpu.make_async_copy(l_ref, lo_ref, init_sem.at[2]),
-        pltpu.make_async_copy(lr_ref, lroot.at[pl.ds(2 * ((y * (side // 2) + x // 2) * CORES + c), 2)], init_sem.at[3]),
+        pltpu.make_async_copy(rr_ref, rr, x_send.at[0]),
+        pltpu.make_async_copy(r_ref, ro_ref, x_send.at[1]),
+        pltpu.make_async_copy(l_ref, lo_ref, d_send.at[0]),
+        pltpu.make_async_copy(lr_ref, lroot.at[pl.ds(2 * ((y * (side // 2) + x // 2) * CORES + c), 2)], l_send.at[0]),
     ]
     own_load = pltpu.make_async_copy(g_ref, gbuf.at[0], load_sem.at[0])
     own_load.start()
@@ -266,12 +266,17 @@
         core = c + p * (1 - 2 * c)
         return (oy * (side // 2) + ox // 2) * CORES + core, (oy * side + ox) * CORES + core
 
+    def twin_turn(place):
+        return g_recv.at[ROUNDS + 1 + place // CORES]
+
+    twin_last = g_recv.at[ROUNDS + 1 + half_count // 4]
+
     def root_copy(peer, place, half, src=None, dst=None, recv=None, part=None, across=0):
         here = lroot.at[2 * place + half]
         if part is not None:
             here = here.at[pl.ds(*pieces[part])]
         if peer is twin and recv is None:
-            recv = l_recv.at[TWIN_TURN + place // CORES]
+            recv = twin_turn(place)
         return pltpu.make_async_remote_copy(
             src_ref=here if src is None else src, dst_ref=here if dst is None else dst, send_sem=l_send.at[across],
             recv_sem=l_recv.at[recv] if isinstance(recv, int) else recv, device_id={"tensor": peer}, device_id_type=MESH)
@@ -348,11 +353,11 @@
     def root_last(part):
         pair_wait(lroot.at[pl.ds(0, 2), pl.ds(*pieces[part])], l_recv.at[LAST_TURN + part])
         for half in (0, 1):
-            root_send(twin, last_place, half, part=part, recv=TWIN_LAST if part else None)
+            root_send(twin, last_place, half, part=part, recv=twin_last if part else None)
 
     def root_last_twin(part):
         pair = lroot.at[pl.ds(2 * twin_place, 2), pl.ds(*pieces[part])]
-        pair_wait(pair, l_recv.at[TWIN_LAST if part else TWIN_TURN + twin_place // CORES])
+        pair_wait(pair, twin_last if part else twin_turn(twin_place))
 
     steps(grad, gbuf, load_sem, GRAD_ROUND_STEP, [(RELAY_STEP, lambda: root_relay(0))],
           [(ROOT_ACROSS_STEP, root_start_across), (ROOT_ACROSS_STEP, lambda: pl.when(c == 1)(lambda: uncounted(root_start)))],
@@ -387,7 +392,7 @@
     def twin_wait(i, place):
         @pl.when(i % 2 == 1)
         def _():
-            pair_wait(lroot.at[pl.ds(2 * place, 2)], l_recv.at[TWIN_TURN + place // CORES])
+            pair_wait(lroot.at[pl.ds(2 * place, 2)], twin_turn(place))
 
     def product(place, which):
         left = lroot[pl.ds(2 * place, 2)].reshape(lrows, rows)
@@ -565,8 +570,7 @@
                 pltpu.SemaphoreType.DMA((ROUNDS + n // 2,)),
                 pltpu.SemaphoreType.DMA((1,)),
                 pltpu.SemaphoreType.DMA((2,)),
-                pltpu.SemaphoreType.DMA((4,)),
-                pltpu.SemaphoreType.DMA((TWIN_TURN + kept // 2,)),
+                pltpu.SemaphoreType.DMA((ROOT_TURNS,)),
                 pltpu.SemaphoreType.DMA((3,)),
                 pltpu.SemaphoreType.DMA((2,)),
                 pltpu.SemaphoreType.DMA((1,)),

time: 253 us -> 253 us (level)
  no operation moved by 1% of the time
where the time goes in v1:
time: 253 us
  Pallas kernels  252 us (100%)
    pallas_call x1, Pallas kernels, local_step(): pl.pallas_call(functools.partial(kernel, n, side), name='shampoo', out_sh...  247 us
    pallas_call x1, Pallas kernels, local_step(): pl.pallas_call(store_kernel, name='store', out_shape=[jax.ShapeDtypeStruc...  5.19 us

profile of v1, /device:TPU:97, one launch (start us, length us, event | category | flops | bytes accessed | tf_op | source)
XLA Modules:
  0.0 252.7 jit_solution(12469664953383004378)
XLA Ops:
  0.6 246.9 %shampoo.1 = (f32[128,4096]{1,0:T(8,128)S(1)}, f32[256,8192]{1,0:T(8,128)S(1)}, f32[4096,256]{1,0:T(8,128)S(1)}, bf16[64,2048,256]{2,1,0:T(8,128)(2,1)}) custom-call(bf16[2,2048,256]{2,1,0:T(8,128)(2,1)} %bitcast.2, f32[128,4096]{1,0:T(8,128)} %l_ref.1, f32[256,8192]{1,0:T(8,128)} %r_ref.1, bf16[2,64,4096]{2,1,0:T(8,128)(2,1)} %bitcast.3, ...), custom_call_target="tpu_custom_call" | custom-call | flops 51539607552 | bytes 201326592 | tf_op jit(solution)/shard_map/shampoo/pallas_call | solution.py:549
  247.5 5.2 %store.1 = (f32[128,4096]{1,0:T(8,128)}, f32[256,8192]{1,0:T(8,128)}, f32[4096,256]{1,0:T(8,128)}) custom-call(f32[128,4096]{1,0:T(8,128)S(1)} %get-tuple-element.6.refs_0_, f32[256,8192]{1,0:T(8,128)S(1)} %get-tuple-element.7.refs_1_, f32[4096,256]{1,0:T(8,128)S(1)} %get-tuple-element.8.refs_2_), custom_call_target="tpu_custom_call" | custom-call | tf_op jit(solution)/shard_map/store/pallas_call | solution.py:586

commit v2 on v1

--- a/solution.py
+++ b/solution.py
@@ -28,7 +28,7 @@
 GRAD_ROUND_STEP = [2, 2, 8, 10, 12, 14, 17, 20, 22, 26, 28, 30]
 LAST_FORWARD = 7
 SIDE_UP, SIDE_DOWN = 9, 10
-ASIDE = 36
+ASIDE = 33
 ROOT_START_STEP = 28
 ROOT_ACROSS_STEP = 30
 RELAY_STEP = 32
@@ -522,7 +522,7 @@
 def store_kernel(*refs):
     count = (len(refs) - 1) // 2
     sems = refs[-1]
-    pieces = 8
+    pieces = 16
     for i in range(count):
         src, dst = refs[i], refs[count + i]
         step = src.shape[0] // pieces

time: 253 us -> 253 us (level)
  no operation moved by 1% of the time
where the time goes in v2:
time: 253 us; the launch traced here: 252 us
  Pallas kernels  252 us (100%)
    pallas_call x1, Pallas kernels, local_step(): pl.pallas_call(functools.partial(kernel, n, side), name='shampoo', out_sh...  247 us
    pallas_call x1, Pallas kernels, local_step(): pl.pallas_call(store_kernel, name='store', out_shape=[jax.ShapeDtypeStruc...  5.17 us

profile of v2, /device:TPU:97, one launch (start us, length us, event | category | flops | bytes accessed | tf_op | source)
XLA Modules:
  0.0 252.4 jit_solution(2519255047073983750)
XLA Ops:
  0.6 246.6 %shampoo.1 = (f32[128,4096]{1,0:T(8,128)S(1)}, f32[256,8192]{1,0:T(8,128)S(1)}, f32[4096,256]{1,0:T(8,128)S(1)}, bf16[64,2048,256]{2,1,0:T(8,128)(2,1)}) custom-call(bf16[2,2048,256]{2,1,0:T(8,128)(2,1)} %bitcast.2, f32[128,4096]{1,0:T(8,128)} %l_ref.1, f32[256,8192]{1,0:T(8,128)} %r_ref.1, bf16[2,64,4096]{2,1,0:T(8,128)(2,1)} %bitcast.3, ...), custom_call_target="tpu_custom_call" | custom-call | flops 51539607552 | bytes 201326592 | tf_op jit(solution)/shard_map/shampoo/pallas_call | solution.py:549
  247.3 5.2 %store.1 = (f32[128,4096]{1,0:T(8,128)}, f32[256,8192]{1,0:T(8,128)}, f32[4096,256]{1,0:T(8,128)}) custom-call(f32[128,4096]{1,0:T(8,128)S(1)} %get-tuple-element.6.refs_0_, f32[256,8192]{1,0:T(8,128)S(1)} %get-tuple-element.7.refs_1_, f32[4096,256]{1,0:T(8,128)S(1)} %get-tuple-element.8.refs_2_), custom_call_target="tpu_custom_call" | custom-call | tf_op jit(solution)/shard_map/store/pallas_call | solution.py:586

commit v3 on v2

--- a/solution.py
+++ b/solution.py
@@ -28,7 +28,7 @@
 GRAD_ROUND_STEP = [2, 2, 8, 10, 12, 14, 17, 20, 22, 26, 28, 30]
 LAST_FORWARD = 7
 SIDE_UP, SIDE_DOWN = 9, 10
-ASIDE = 33
+ASIDE = {"+": 29, "-": 37}
 ROOT_START_STEP = 28
 ROOT_ACROSS_STEP = 30
 RELAY_STEP = 32
@@ -67,7 +67,7 @@
     rows = 2 * half_rows
     lrows = l_ref.shape[0]
     tile = min(1024, half_rows)
-    aside_rows = half_rows * ASIDE // 128
+    aside_rows = {way: half_rows * share // 128 for way, share in ASIDE.items()}
 
     me = lax.axis_index("tensor")
     c = me % CORES
@@ -150,11 +150,12 @@
 
         def forward_last(self, name, offset, half):
             self.sent += 1
-            pl.when(c == 0)(lambda: self.copy(name, offset, half, part=(0, half_rows - aside_rows)).start())
+            pl.when(c == 0)(lambda: self.copy(name, offset, half, part=(0, half_rows - aside_rows[name[1]])).start())
             pl.when(c == 1)(lambda: self.copy(name, offset, half).start())
 
         def aside(self, name, offset, half):
-            part = (half_rows - aside_rows, aside_rows)
+            count = aside_rows[name[1]]
+            part = (half_rows - count, count)
             pl.when(c == 0)(lambda: self.copy(name, offset, half, part=part, turn=ROUNDS - 1).start())
 
         def drain(self):
@@ -221,11 +222,11 @@
     ]
     own_load = pltpu.make_async_copy(g_ref, gbuf.at[0], load_sem.at[0])
     own_load.start()
+    for copy in first:
+        copy.start()
 
     pl.semaphore_wait(barrier, len(peers))
     grad.start()
-    for copy in first:
-        copy.start()
 
     acc[...] = jnp.zeros_like(acc)
     own_load.wait()
@@ -522,7 +523,7 @@
 def store_kernel(*refs):
     count = (len(refs) - 1) // 2
     sems = refs[-1]
-    pieces = 16
+    pieces = 32
     for i in range(count):
         src, dst = refs[i], refs[count + i]
         step = src.shape[0] // pieces

time: 253 us -> 253 us (level)
  no operation moved by 1% of the time
where the time goes in v3:
time: 253 us
  Pallas kernels  252 us (100%)
    pallas_call x1, Pallas kernels, local_step(): pl.pallas_call(functools.partial(kernel, n, side), name='shampoo', out_sh...  247 us
    pallas_call x1, Pallas kernels, local_step(): pl.pallas_call(store_kernel, name='store', out_shape=[jax.ShapeDtypeStruc...  5.14 us

profile of v3, /device:TPU:97, one launch (start us, length us, event | category | flops | bytes accessed | tf_op | source)
XLA Modules:
  0.0 253.1 jit_solution(185748657753185882)
XLA Ops:
  0.6 247.3 %shampoo.1 = (f32[128,4096]{1,0:T(8,128)S(1)}, f32[256,8192]{1,0:T(8,128)S(1)}, f32[4096,256]{1,0:T(8,128)S(1)}, bf16[64,2048,256]{2,1,0:T(8,128)(2,1)}) custom-call(bf16[2,2048,256]{2,1,0:T(8,128)(2,1)} %bitcast.2, f32[128,4096]{1,0:T(8,128)} %l_ref.1, f32[256,8192]{1,0:T(8,128)} %r_ref.1, bf16[2,64,4096]{2,1,0:T(8,128)(2,1)} %bitcast.3, ...), custom_call_target="tpu_custom_call" | custom-call | flops 51539607552 | bytes 201326592 | tf_op jit(solution)/shard_map/shampoo/pallas_call | solution.py:550
  248.0 5.1 %store.1 = (f32[128,4096]{1,0:T(8,128)}, f32[256,8192]{1,0:T(8,128)}, f32[4096,256]{1,0:T(8,128)}) custom-call(f32[128,4096]{1,0:T(8,128)S(1)} %get-tuple-element.6.refs_0_, f32[256,8192]{1,0:T(8,128)S(1)} %get-tuple-element.7.refs_1_, f32[4096,256]{1,0:T(8,128)S(1)} %get-tuple-element.8.refs_2_), custom_call_target="tpu_custom_call" | custom-call | tf_op jit(solution)/shard_map/store/pallas_call | solution.py:587

commit v4 on v3

--- a/solution.py
+++ b/solution.py
@@ -28,7 +28,7 @@
 GRAD_ROUND_STEP = [2, 2, 8, 10, 12, 14, 17, 20, 22, 26, 28, 30]
 LAST_FORWARD = 7
 SIDE_UP, SIDE_DOWN = 9, 10
-ASIDE = {"+": 29, "-": 37}
+ASIDE = {"+": 33, "-": 33}
 ROOT_START_STEP = 28
 ROOT_ACROSS_STEP = 30
 RELAY_STEP = 32

time: 253 us -> 253 us (level)
  no operation moved by 1% of the time
where the time goes in v4:
time: 253 us; the launch traced here: 252 us
  Pallas kernels  252 us (100%)
    pallas_call x1, Pallas kernels, local_step(): pl.pallas_call(functools.partial(kernel, n, side), name='shampoo', out_sh...  247 us
    pallas_call x1, Pallas kernels, local_step(): pl.pallas_call(store_kernel, name='store', out_shape=[jax.ShapeDtypeStruc...  5.14 us

profile of v4, /device:TPU:97, one launch (start us, length us, event | category | flops | bytes accessed | tf_op | source)
XLA Modules:
  0.0 252.4 jit_solution(2693592617549364529)
XLA Ops:
  0.6 246.6 %shampoo.1 = (f32[128,4096]{1,0:T(8,128)S(1)}, f32[256,8192]{1,0:T(8,128)S(1)}, f32[4096,256]{1,0:T(8,128)S(1)}, bf16[64,2048,256]{2,1,0:T(8,128)(2,1)}) custom-call(bf16[2,2048,256]{2,1,0:T(8,128)(2,1)} %bitcast.2, f32[128,4096]{1,0:T(8,128)} %l_ref.1, f32[256,8192]{1,0:T(8,128)} %r_ref.1, bf16[2,64,4096]{2,1,0:T(8,128)(2,1)} %bitcast.3, ...), custom_call_target="tpu_custom_call" | custom-call | flops 51539607552 | bytes 201326592 | tf_op jit(solution)/shard_map/shampoo/pallas_call | solution.py:550
  247.3 5.1 %store.1 = (f32[128,4096]{1,0:T(8,128)}, f32[256,8192]{1,0:T(8,128)}, f32[4096,256]{1,0:T(8,128)}) custom-call(f32[128,4096]{1,0:T(8,128)S(1)} %get-tuple-element.6.refs_0_, f32[256,8192]{1,0:T(8,128)S(1)} %get-tuple-element.7.refs_1_, f32[4096,256]{1,0:T(8,128)S(1)} %get-tuple-element.8.refs_2_), custom_call_target="tpu_custom_call" | custom-call | tf_op jit(solution)/shard_map/store/pallas_call | solution.py:587

commit v5 on v4

--- a/solution.py
+++ b/solution.py
@@ -360,8 +360,8 @@
         pair = lroot.at[pl.ds(2 * twin_place, 2), pl.ds(*pieces[part])]
         pair_wait(pair, twin_last if part else twin_turn(twin_place))
 
-    steps(grad, gbuf, load_sem, GRAD_ROUND_STEP, [(RELAY_STEP, lambda: root_relay(0))],
-          [(ROOT_ACROSS_STEP, root_start_across), (ROOT_ACROSS_STEP, lambda: pl.when(c == 1)(lambda: uncounted(root_start)))],
+    steps(grad, gbuf, load_sem, GRAD_ROUND_STEP, [(RELAY_STEP, lambda: root_relay(0)), (ROOT_ACROSS_STEP, lambda: pl.when(c == 1)(lambda: uncounted(root_start)))],
+          [(ROOT_ACROSS_STEP, root_start_across)],
           [(ROOT_START_STEP, lambda: pl.when(c == 0)(root_start))], grad_work)
 
     side_cols = cols // 2

time: 253 us -> 253 us (level)
  no operation moved by 1% of the time
where the time goes in v5:
time: 253 us; the launch traced here: 252 us
  Pallas kernels  252 us (100%)
    pallas_call x1, Pallas kernels, local_step(): pl.pallas_call(functools.partial(kernel, n, side), name='shampoo', out_sh...  247 us
    pallas_call x1, Pallas kernels, local_step(): pl.pallas_call(store_kernel, name='store', out_shape=[jax.ShapeDtypeStruc...  5.14 us

profile of v5, /device:TPU:97, one launch (start us, length us, event | category | flops | bytes accessed | tf_op | source)
XLA Modules:
  0.0 252.4 jit_solution(15855762128679364791)
XLA Ops:
  0.6 246.6 %shampoo.1 = (f32[128,4096]{1,0:T(8,128)S(1)}, f32[256,8192]{1,0:T(8,128)S(1)}, f32[4096,256]{1,0:T(8,128)S(1)}, bf16[64,2048,256]{2,1,0:T(8,128)(2,1)}) custom-call(bf16[2,2048,256]{2,1,0:T(8,128)(2,1)} %bitcast.2, f32[128,4096]{1,0:T(8,128)} %l_ref.1, f32[256,8192]{1,0:T(8,128)} %r_ref.1, bf16[2,64,4096]{2,1,0:T(8,128)(2,1)} %bitcast.3, ...), custom_call_target="tpu_custom_call" | custom-call | flops 51539607552 | bytes 201326592 | tf_op jit(solution)/shard_map/shampoo/pallas_call | solution.py:550
  247.3 5.1 %store.1 = (f32[128,4096]{1,0:T(8,128)}, f32[256,8192]{1,0:T(8,128)}, f32[4096,256]{1,0:T(8,128)}) custom-call(f32[128,4096]{1,0:T(8,128)S(1)} %get-tuple-element.6.refs_0_, f32[256,8192]{1,0:T(8,128)S(1)} %get-tuple-element.7.refs_1_, f32[4096,256]{1,0:T(8,128)S(1)} %get-tuple-element.8.refs_2_), custom_call_target="tpu_custom_call" | custom-call | tf_op jit(solution)/shard_map/store/pallas_call | solution.py:587

commit v6 on v4

--- a/solution.py
+++ b/solution.py
@@ -28,7 +28,7 @@
 GRAD_ROUND_STEP = [2, 2, 8, 10, 12, 14, 17, 20, 22, 26, 28, 30]
 LAST_FORWARD = 7
 SIDE_UP, SIDE_DOWN = 9, 10
-ASIDE = {"+": 33, "-": 33}
+ASIDE = {"+": 35, "-": 31}
 ROOT_START_STEP = 28
 ROOT_ACROSS_STEP = 30
 RELAY_STEP = 32

time: 253 us -> 253 us (level)
  no operation moved by 1% of the time
where the time goes in v6:
time: 253 us
  Pallas kernels  252 us (100%)
    pallas_call x1, Pallas kernels, local_step(): pl.pallas_call(functools.partial(kernel, n, side), name='shampoo', out_sh...  247 us
    pallas_call x1, Pallas kernels, local_step(): pl.pallas_call(store_kernel, name='store', out_shape=[jax.ShapeDtypeStruc...  5.14 us

profile of v6, /device:TPU:97, one launch (start us, length us, event | category | flops | bytes accessed | tf_op | source)
XLA Modules:
  0.0 252.6 jit_solution(17330478342569329736)
XLA Ops:
  0.6 246.8 %shampoo.1 = (f32[128,4096]{1,0:T(8,128)S(1)}, f32[256,8192]{1,0:T(8,128)S(1)}, f32[4096,256]{1,0:T(8,128)S(1)}, bf16[64,2048,256]{2,1,0:T(8,128)(2,1)}) custom-call(bf16[2,2048,256]{2,1,0:T(8,128)(2,1)} %bitcast.2, f32[128,4096]{1,0:T(8,128)} %l_ref.1, f32[256,8192]{1,0:T(8,128)} %r_ref.1, bf16[2,64,4096]{2,1,0:T(8,128)(2,1)} %bitcast.3, ...), custom_call_target="tpu_custom_call" | custom-call | flops 51539607552 | bytes 201326592 | tf_op jit(solution)/shard_map/shampoo/pallas_call | solution.py:550
  247.4 5.1 %store.1 = (f32[128,4096]{1,0:T(8,128)}, f32[256,8192]{1,0:T(8,128)}, f32[4096,256]{1,0:T(8,128)}) custom-call(f32[128,4096]{1,0:T(8,128)S(1)} %get-tuple-element.6.refs_0_, f32[256,8192]{1,0:T(8,128)S(1)} %get-tuple-element.7.refs_1_, f32[4096,256]{1,0:T(8,128)S(1)} %get-tuple-element.8.refs_2_), custom_call_target="tpu_custom_call" | custom-call | tf_op jit(solution)/shard_map/store/pallas_call | solution.py:587

commit v7 on v4

--- a/solution.py
+++ b/solution.py
@@ -314,11 +314,11 @@
     def root_relay(half):
         root_copy(helper, own_place, half, src=lr_ref.at[half], dst=relay.at[half], recv=relay_recv.at[half]).wait_recv()
         root_send(helper, passing, half, across=1, src=relay.at[half], recv=FAR_TURN + half)
-        root_send(twin, passing, half, across=1, src=relay.at[half], dst=relay.at[2 + half], recv=relay_recv.at[2])
+        root_send(twin, passing, half, across=1, src=relay.at[half], dst=relay.at[2 + half], recv=g_recv.at[ROUNDS + 10])
 
     def passed_rows(p):
         if p:
-            pair_wait(relay.at[pl.ds(2, 2)], relay_recv.at[2])
+            pair_wait(relay.at[pl.ds(2, 2)], g_recv.at[ROUNDS + 10])
         source = (y * side + (x - (1 - 2 * p) * dx + side) % side) * CORES + c + p * (1 - 2 * c)
         left = relay[2 * p:2 * p + 2].reshape(lrows, rows)
         do_ref[rows_of(source), :] = jnp.dot(left, xx[0], preferred_element_type=jnp.float32)
@@ -572,7 +572,7 @@
                 pltpu.SemaphoreType.DMA((1,)),
                 pltpu.SemaphoreType.DMA((2,)),
                 pltpu.SemaphoreType.DMA((ROOT_TURNS,)),
-                pltpu.SemaphoreType.DMA((3,)),
+                pltpu.SemaphoreType.DMA((2,)),
                 pltpu.SemaphoreType.DMA((2,)),
                 pltpu.SemaphoreType.DMA((1,)),
                 pltpu.SemaphoreType.DMA((2,)),

time: 253 us -> 253 us (level)
  no operation moved by 1% of the time
where the time goes in v7:
time: 253 us; the launch traced here: 252 us
  Pallas kernels  252 us (100%)
    pallas_call x1, Pallas kernels, local_step(): pl.pallas_call(functools.partial(kernel, n, side), name='shampoo', out_sh...  247 us
    pallas_call x1, Pallas kernels, local_step(): pl.pallas_call(store_kernel, name='store', out_shape=[jax.ShapeDtypeStruc...  5.14 us

profile of v7, /device:TPU:97, one launch (start us, length us, event | category | flops | bytes accessed | tf_op | source)
XLA Modules:
  0.0 252.4 jit_solution(2791987962928403340)
XLA Ops:
  0.6 246.6 %shampoo.1 = (f32[128,4096]{1,0:T(8,128)S(1)}, f32[256,8192]{1,0:T(8,128)S(1)}, f32[4096,256]{1,0:T(8,128)S(1)}, bf16[64,2048,256]{2,1,0:T(8,128)(2,1)}) custom-call(bf16[2,2048,256]{2,1,0:T(8,128)(2,1)} %bitcast.2, f32[128,4096]{1,0:T(8,128)} %l_ref.1, f32[256,8192]{1,0:T(8,128)} %r_ref.1, bf16[2,64,4096]{2,1,0:T(8,128)(2,1)} %bitcast.3, ...), custom_call_target="tpu_custom_call" | custom-call | flops 51539607552 | bytes 201326592 | tf_op jit(solution)/shard_map/shampoo/pallas_call | solution.py:550
  247.3 5.1 %store.1 = (f32[128,4096]{1,0:T(8,128)}, f32[256,8192]{1,0:T(8,128)}, f32[4096,256]{1,0:T(8,128)}) custom-call(f32[128,4096]{1,0:T(8,128)S(1)} %get-tuple-element.6.refs_0_, f32[256,8192]{1,0:T(8,128)S(1)} %get-tuple-element.7.refs_1_, f32[4096,256]{1,0:T(8,128)S(1)} %get-tuple-element.8.refs_2_), custom_call_target="tpu_custom_call" | custom-call | tf_op jit(solution)/shard_map/store/pallas_call | solution.py:587
